TPU v7x, 32 devices: a whole 2x2x4 slice. The times are simulated.
32 devices in a mesh: mp: 8 (over z, y), rows: 4 (over x, core).
Axes of the slice: x: 2, y: 2, z: 4, core: 2. Of those that a mesh axis runs over, the one named last changes fastest.
Arguments:
- inputs: float32 [1024, 16384], P('rows', 'mp'), may hold values from -6 to 6
- weight: float32 [512, 16384], P('mp'), may hold values from -1.5 to 1.5, as said below
Outputs:
- row_scale: float32 [1024], P('rows')
- product: float32 [512, 1024], P('mp', 'rows')
- normalized: float32 [512, 1024], P('mp')
Inputs may be any that keep to these rules, and one draw needn't show every extreme that they name: A weight matrix whose rows carry different scales.
All inputs are finite; a program needn't handle non-finite values. Where the computation divides by a largest or mean magnitude, that divisor is 1e-20 or more.
Results may differ from a plain program's by a relative error of at most 0.0003.
Values may be sent and summed in bfloat16 or wider, within the bound.
A program may use at most 64 MiB of HBM per device.

v0:
```python
import jax
import jax.numpy as jnp
from jax import lax
from jax.sharding import PartitionSpec as P

epsilon = 1e-06


def split_two(values):
    scaled = values * 128.0
    first = jnp.floor(scaled)
    second = jnp.floor((scaled - first) * 256.0)
    return (first.astype(jnp.bfloat16), second.astype(jnp.bfloat16))


def matmul(w_side, x_side):
    return lax.dot_general(
        w_side, x_side, (((1,), (1,)), ((), ())), preferred_element_type=jnp.float32
    )


def pair_sums(x_parts, w_parts):
    level_zero = matmul(w_parts[0], x_parts[0])
    level_one = matmul(w_parts[0], x_parts[1]) + matmul(w_parts[1], x_parts[0])
    return (level_zero, level_one)


def combine_levels(levels):
    return levels[0] + levels[1] / 256.0


def per_device(inputs, weight):
    col_scale = jnp.max(jnp.abs(weight), axis=1) + epsilon
    w_parts = split_two(weight / col_scale[:, None])
    row_scale = lax.pmax(jnp.max(jnp.abs(inputs), axis=1), "mp") + epsilon
    x_parts = split_two(inputs / row_scale[:, None])
    stacked = jnp.stack(w_parts, axis=0)
    moved = lax.all_to_all(stacked, "mp", split_axis=2, concat_axis=1, tiled=True)
    partial_term = combine_levels(pair_sums(x_parts, (moved[0], moved[1])))
    combined = lax.psum_scatter(partial_term, "mp", scatter_dimension=0, tiled=True)
    product = combined * col_scale[:, None] * row_scale[None, :] / 16384.0
    squares = lax.psum(jnp.sum(product * product, axis=0), "mp")
    mean_square = squares / (weight.shape[0] * lax.axis_size("mp"))
    normalized = product * lax.rsqrt(mean_square + epsilon)[None, :]
    gathered_rows = lax.all_gather(normalized, "rows", axis=1, tiled=True)
    return (row_scale, product, gathered_rows)


def solution(mesh):
    return jax.shard_map(
        per_device,
        mesh=mesh,
        in_specs=(P("rows", "mp"), P("mp", None)),
        out_specs=(P("rows"), P("mp", "rows"), P("mp", None)),
        check_vma=False,
    )
```

profile of v0, /device:TPU:0, one launch (start us, length us, event | category | flops | bytes accessed | tf_op | source)
XLA Modules:
  0.0 281.4 jit_solution(13112939245431465066)
XLA Ops:
  7.2 0.0 copy-start
  7.2 2.6 abs_reduce_fusion
  9.8 0.8 copy-done
  10.6 1.1 fusion.7
  11.7 2.3 pad_maximum_fusion
  14.0 17.8 %copy.12 = bf16[2,64,16384]{1,0,2:T(2,128)(2,1)} copy(bf16[2,64,16384]{2,1,0:T(8,128)(2,1)} %pad_maximum_fusion) | data formatting | bytes 8388608 | tf_op jit(solution)/shard_map/stack | solution.py:37
  31.8 10.5 %reshape.16 = bf16[8,2,131072]{2,1,0:T(2,128)(2,1)} reshape(bf16[16384,2,64]{2,1,0:T(2,128)(2,1)} %bitcast.13) | data formatting | bytes 8388608
  42.3 0.0 copy-start.1
  42.3 7.4 %all-to-all-start = ((bf16[8,2,131072]{2,1,0:T(2,128)(2,1)}), bf16[8,2,131072]{2,1,0:T(2,128)(2,1)}, u32[]{:S(2)}, u32[]{:S(2)}) async-start(bf16[8,2,131072]{2,1,0:T(2,128)(2,1)} %reshape.16), calls=%async_computation | async-start | bytes 8388608 | tf_op jit(solution)/shard_map/all_to_all | solution.py:38
  49.7 0.0 reduce-scatter.2.cloned.1.call-start
  49.8 0.0 copy-done.1
  49.8 0.2 abs_reduce_fusion.1
  50.0 85.0 %pmax.7 = f32[256]{0:T(256)S(1)} all-reduce(f32[256]{0:T(256)S(1)} %abs_reduce_fusion.1), channel_id=1, replica_groups=mesh['mp'=8,'rows'=4] {'mp'}, use_global_device_ids=true, to_apply=%region_1.0 | all-reduce | flops 256 | bytes 2048 | tf_op jit(solution)/shard_map/pmax | solution.py:35
  135.0 0.0 copy-start.2
  135.0 8.1 %all-to-all-done = bf16[8,2,131072]{2,1,0:T(2,128)(2,1)} async-done(((bf16[8,2,131072]{2,1,0:T(2,128)(2,1)}), bf16[8,2,131072]{2,1,0:T(2,128)(2,1)}, u32[]{:S(2)}, u32[]{:S(2)}) %all-to-all-start) | async-done | bytes 4194336 | tf_op jit(solution)/shard_map/all_to_all | solution.py:38
  143.1 10.3 %reshape.17 = bf16[16384,2,64]{2,1,0:T(2,128)(2,1)} reshape(bf16[8,2,131072]{2,1,0:T(2,128)(2,1)} %all-to-all-done) | data formatting | bytes 8388608
  153.4 13.6 %copy.16 = bf16[2,64,8,2048]{3,2,1,0:T(8,128)(2,1)} copy(bf16[2,64,8,2048]{1,0,3,2:T(2,128)(2,1)} %bitcast.14) | data formatting | bytes 8388608 | tf_op jit(solution)/shard_map/all_to_all | solution.py:38
  167.0 2.7 fusion.16
  169.7 1.2 copy.14
  170.9 1.2 copy.15
  172.1 1.0 fusion.9
  173.1 0.9 fusion.8
  174.0 1.7 convolution_add_fusion.1
  175.6 0.0 reduce-scatter.2.cloned.1.call-update
  175.6 70.5 %reduce-scatter.2.cloned.1.call-done = f32[64,256]{1,0:T(8,128)} async-done(((f32[512,256]{1,0:T(8,128)}), f32[64,256]{1,0:T(8,128)}) %reduce-scatter.2.cloned.1.call-update) | async-done | bytes 65552 | tf_op jit(solution)/shard_map/reduce_scatter | solution.py:40
  246.1 1.6 multiply_reduce_fusion
  247.7 19.4 %psum.7 = f32[256]{0:T(256)S(1)} all-reduce(f32[256]{0:T(256)S(1)} %get-tuple-element.3), channel_id=1, replica_groups=mesh['mp'=8,'rows'=4] {'mp'}, use_global_device_ids=true, to_apply=%region_5.0 | all-reduce | flops 256 | bytes 2048 | tf_op jit(solution)/shard_map/psum | solution.py:42
  267.1 0.0 copy-done.2
  267.1 0.9 fusion.12
  268.0 5.8 %all_gather.3 = f32[64,1024]{1,0:T(8,128)S(1)} all-gather(f32[64,256]{1,0:T(8,128)S(1)} %fusion.12), channel_id=1, replica_groups=mesh['mp'=8,'rows'=4] {'rows'}, dimensions={1}, use_global_device_ids=true | all-gather | bytes 327680 | tf_op jit(solution)/shard_map/all_gather | solution.py:45
  273.8 0.7 copy.18
  (3 shorter events, 0.0 us)
Async XLA Ops:
  7.2 3.5 %copy-start = (f32[64,16384]{1,0:T(8,128)S(1)}, f32[64,16384]{1,0:T(8,128)}, u32[]{:S(2)}) copy-start(f32[64,16384]{1,0:T(8,128)} %param.3) | copy-start | bytes 12582916
  42.3 7.5 %copy-start.1 = (f32[256,2048]{1,0:T(8,128)S(1)}, f32[256,2048]{1,0:T(8,128)}, u32[]{:S(2)}) copy-start(f32[256,2048]{1,0:T(8,128)} %param.2) | copy-start | bytes 6291460
  42.3 100.8 %all-to-all-start = ((bf16[8,2,131072]{2,1,0:T(2,128)(2,1)}), bf16[8,2,131072]{2,1,0:T(2,128)(2,1)}, u32[]{:S(2)}, u32[]{:S(2)}) async-start(bf16[8,2,131072]{2,1,0:T(2,128)(2,1)} %reshape.16), calls=%async_computation | async-start | bytes 8388608 | tf_op jit(solution)/shard_map/all_to_all | solution.py:38
  49.7 196.4 %reduce-scatter.2.cloned.1.call-start = ((), (), s32[]{:S(2)}) async-start(), calls=%async_computation.2 | async-start | bytes 589824 | tf_op jit(solution)/shard_map/reduce_scatter | solution.py:40
  135.0 132.1 %copy-start.2 = (f32[256]{0:T(256)}, f32[256]{0:T(256)S(1)}, u32[]{:S(2)}) copy-start(f32[256]{0:T(256)S(1)} %broadcast_add_fusion) | copy-start | bytes 3076
Sparse Core Ops, SparseCore 0:
  175.8 70.3 reduce-scatter.1
where the time goes:
time: 283 us; the launch traced here: 281 us
  blocking collectives  110 us (39%)
  waiting for transfers between devices  78.6 us (28%)
  local copies, waits for them, and re-layouts  58.7 us (21%)
  between operations  14.1 us (5%)
  other arithmetic  8.76 us (3%)
  starting transfers between devices  7.48 us (3%)
  matrix products  3.54 us (1%)
    pmax x1, blocking collectives, per_device(): row_scale = lax.pmax(jnp.max(jnp.abs(inputs), axis=1), 'mp') + epsilon  85 us
    reduce_scatter x1, waiting for transfers between devices, per_device(): lax.psum_scatter(partial_term, 'mp', scatter_dimension=0, tiled=True)  70.5 us
    unnamed x9, local copies, waits for them, and re-layouts  22.3 us
    psum x1, blocking collectives, per_device(): squares = lax.psum(jnp.sum(product * product, axis=0), 'mp')  19.4 us
    another operation x1, local copies, waits for them, and re-layouts, per_device(): stacked = jnp.stack(w_parts, axis=0)  17.8 us
    all_to_all x1, local copies, waits for them, and re-layouts, per_device(): lax.all_to_all(stacked, 'mp', split_axis=2, concat_axis=1, tiled=True)  13.6 us
    all_to_all x1, waiting for transfers between devices, per_device(): lax.all_to_all(stacked, 'mp', split_axis=2, concat_axis=1, tiled=True)  8.12 us
    all_to_all x1, starting transfers between devices, per_device(): lax.all_to_all(stacked, 'mp', split_axis=2, concat_axis=1, tiled=True)  7.44 us
  transfers between devices with their start and end apart: 2, of which 2 were waited for; matrix products, arithmetic and copies ran while one was open for 0% of the time, Pallas kernels for 0%

commit v1 on v0

v1 whole, which is shorter than its diff:
```python
import functools

import jax
import jax.numpy as jnp
from jax import lax
from jax.experimental import pallas as pl
from jax.experimental.pallas import tpu as pltpu
from jax.sharding import PartitionSpec as P

epsilon = 1e-06
MESH = pl.DeviceIdType.MESH


def partner(me, step, count):
    if count & (count - 1):
        return lax.rem(step - me + count, count)
    out, bit = 0, 1
    while bit < count:
        out = out + bit * lax.rem(lax.div(me, bit) + lax.div(step, bit), 2)
        bit *= 2
    return out


def kernel(n_mp, n_rows, x_hbm, w_hbm, scale_out, product_out, norm_out,
           wq, wv, xv, sbuf, wbuf, xparts, xmax, psend, pbuf, gbuf, ssq, cscale,
           load_sem, z_send, z_recv, a_send, a_recv, b_send, b_recv,
           m_send, m_recv, p_send, p_recv, g_send, g_recv, q_send, q_recv):
    me, row = lax.axis_index("mp"), lax.axis_index("rows")
    n_b = 2 if n_rows % 2 == 0 else 1
    n_a = n_rows // n_b
    a, b = lax.div(row, n_b), lax.rem(row, n_b)
    total = n_mp * n_rows
    here = me * n_rows + row
    cols, inner_all = wv.shape
    rows, inner = xv.shape
    quarter = cols // n_rows

    def load(src, dst, at):
        return pltpu.make_async_copy(src, dst, load_sem.at[at])

    load_q = load(w_hbm.at[pl.ds(pl.multiple_of(row * quarter, quarter), quarter)], wq, 0)
    load_x = load(x_hbm, xv, 1)
    load_w = load(w_hbm, wv, 2)
    load_q.start()
    load_x.start()
    load_w.start()

    barrier = pltpu.get_barrier_semaphore()

    def greet(i, carry):
        to = lax.rem(here + i, total)
        pl.semaphore_signal(barrier, inc=1,
                            device_id={"mp": lax.div(to, n_rows), "rows": lax.rem(to, n_rows)},
                            device_id_type=MESH)
        return carry

    lax.fori_loop(1, total, greet, 0)

    load_q.wait()

    def block(i):
        return pl.ds(pl.multiple_of(i * inner, inner), inner)

    def widest(i, top):
        return jnp.maximum(top, jnp.max(jnp.abs(wq[:, block(i)]), axis=1, keepdims=True))

    top = lax.fori_loop(0, n_mp, widest, jnp.zeros((quarter, 1), jnp.float32)) + epsilon

    def cut(i, carry):
        t = wq[:, block(i)] / top * 128.0
        first = jnp.floor(t)
        sbuf[i, 0] = first.astype(jnp.bfloat16)
        sbuf[i, 1] = jnp.floor((t - first) * 256.0).astype(jnp.bfloat16)
        return carry

    lax.fori_loop(0, n_mp, cut, 0)

    def piece(who, at):
        return wbuf.at[who, :, pl.ds(pl.multiple_of(at * quarter, quarter), quarter), :]

    wbuf[me, :, pl.ds(pl.multiple_of(row * quarter, quarter), quarter), :] = sbuf[me]

    pl.semaphore_wait(barrier, total - 1)

    def remote(src, dst, send, recv, **where):
        return pltpu.make_async_remote_copy(src_ref=src, dst_ref=dst, send_sem=send, recv_sem=recv,
                                            device_id=where, device_id_type=MESH)

    def send_block(i, carry):
        to = partner(me, i, n_mp)

        @pl.when(to != me)
        def _():
            remote(sbuf.at[to], piece(me, row), z_send, z_recv.at[me], mp=to).start()
        return carry

    steps = lambda: (1, n_mp) if not (n_mp & (n_mp - 1)) else (0, n_mp)
    lax.fori_loop(*steps(), send_block, 0)

    def peer_a(k):
        return lax.rem(a + k, n_a) * n_b + b

    def peer_b(k):
        return a * n_b + lax.rem(b + k, n_b)

    def spread(who):
        for k in range(1, n_a):
            remote(piece(who, row), piece(who, row), a_send.at[k - 1],
                   a_recv.at[k - 1, who], rows=peer_a(k)).start()
        for k in range(1, n_b):
            remote(piece(who, row), piece(who, row), b_send.at[(k - 1) * n_a],
                   b_recv.at[(k - 1) * n_a, who], rows=peer_b(k)).start()

    spread(me)

    load_x.wait()
    lanes = 128
    peak = jnp.zeros((rows, lanes), jnp.float32)
    for j in range(inner // lanes):
        peak = jnp.maximum(peak, jnp.abs(xv[:, j * lanes:(j + 1) * lanes]))
    xmax[me] = jnp.max(peak.T, axis=0, keepdims=True)

    def tell(i, carry):
        to = lax.rem(me + i, n_mp)
        remote(xmax.at[me], xmax.at[me], m_send, m_recv, mp=to).start()
        return carry

    lax.fori_loop(1, n_mp, tell, 0)

    load_w.wait()
    big = jnp.zeros((cols, lanes), jnp.float32)

    def widest_all(i, big):
        at = pl.multiple_of(i * inner, inner)
        for j in range(inner // lanes):
            big = jnp.maximum(big, jnp.abs(wv[:, pl.ds(at + j * lanes, lanes)]))
        return big

    big = lax.fori_loop(0, n_mp, widest_all, big)
    cscale[...] = jnp.broadcast_to(jnp.max(big, axis=1, keepdims=True) + epsilon, (cols, lanes))

    def slices_of_x():
        remote(xmax.at[pl.ds(0, n_mp - 1)], xmax.at[pl.ds(0, n_mp - 1)], m_send, m_recv, mp=me).wait_recv()
        row_scale = jnp.max(xmax[...], axis=0) + epsilon
        scale_out[...] = row_scale
        tall = jnp.broadcast_to(row_scale, (lanes, rows)).T
        for j in range(inner // lanes):
            at = slice(j * lanes, (j + 1) * lanes)
            t = xv[:, at] / tall * 128.0
            first = jnp.floor(t)
            xparts[0, :, at] = first.astype(jnp.bfloat16)
            xparts[1, :, at] = jnp.floor((t - first) * 256.0).astype(jnp.bfloat16)

    def dot(w_side, x_side):
        return lax.dot_general(w_side, x_side, (((1,), (1,)), ((), ())),
                               preferred_element_type=jnp.float32)

    def stage(i, carry):
        @pl.when(i < n_mp)
        def _():
            who = partner(me, i, n_mp) if not (n_mp & (n_mp - 1)) else lax.rem(me + i, n_mp)

            @pl.when(i > 0)
            def _():
                remote(piece(who, row), piece(who, row), z_send, z_recv.at[who], mp=me).wait_recv()
                spread(who)

        @pl.when((i >= 1) & (i < n_mp + 1))
        def _():
            who = partner(me, i - 1, n_mp) if not (n_mp & (n_mp - 1)) else lax.rem(me + i - 1, n_mp)
            for k in range(1, n_a):
                got = piece(who, lax.rem(a - k + n_a, n_a) * n_b + b)
                remote(got, got, a_send.at[k - 1], a_recv.at[k - 1, who], mp=me).wait_recv()
                for kb in range(1, n_b):
                    at = (kb - 1) * n_a + k
                    remote(got, got, b_send.at[at], b_recv.at[at, who], rows=peer_b(kb)).start()

        @pl.when(i == 2)
        def _():
            slices_of_x()

        @pl.when(i >= 2)
        def _():
            who = partner(me, i - 2, n_mp) if not (n_mp & (n_mp - 1)) else lax.rem(me + i - 2, n_mp)
            for kb in range(1, n_b):
                other_b = lax.rem(b - kb + n_b, n_b)
                for k in range(n_a):
                    at = (kb - 1) * n_a + k
                    got = piece(who, lax.rem(a - k + n_a, n_a) * n_b + other_b)
                    remote(got, got, b_send.at[at], b_recv.at[at, who], mp=me).wait_recv()
            pair = dot(wbuf[who].reshape(2 * cols, inner), xparts[0])
            cross = dot(wbuf[who, 0], xparts[1])
            psend[who] = pair[:cols] + (pair[cols:] + cross) / 256.0

            @pl.when(who != me)
            def _():
                remote(psend.at[who], pbuf.at[me], p_send, p_recv, mp=who).start()

            @pl.when(who == me)
            def _():
                pbuf[me] = psend[me]
        return carry

    lax.fori_loop(0, n_mp + 2, stage, 0)

    remote(pbuf.at[pl.ds(0, n_mp - 1)], pbuf.at[pl.ds(0, n_mp - 1)], p_send, p_recv, mp=me).wait_recv()
    summed = lax.fori_loop(0, n_mp, lambda i, acc: acc + pbuf[i], jnp.zeros((cols, rows), jnp.float32))
    product = summed * cscale[:, :1] * scale_out[...] / float(inner_all)
    gbuf[row] = product
    ssq[here] = jnp.sum(product * product, axis=0, keepdims=True)

    for k in range(1, n_rows):
        remote(gbuf.at[row], gbuf.at[row], g_send, g_recv.at[k - 1], rows=lax.rem(row + k, n_rows)).start()

    def share(i, carry):
        to = lax.rem(here + i, total)
        remote(ssq.at[here], ssq.at[here], q_send, q_recv,
               mp=lax.div(to, n_rows), rows=lax.rem(to, n_rows)).start()
        return carry

    lax.fori_loop(1, total, share, 0)
    product_out[...] = product
    everyone = ssq.at[pl.ds(0, total - 1)]
    remote(everyone, everyone, q_send, q_recv, mp=me).wait_recv()

    for k in range(n_rows):
        src = lax.rem(row - k + n_rows, n_rows)
        if k:
            remote(gbuf.at[src], gbuf.at[src], g_send, g_recv.at[k - 1], mp=me).wait_recv()
        squares = lax.fori_loop(0, n_mp, lambda i, acc: acc + ssq[i * n_rows + src],
                                jnp.zeros((1, rows), jnp.float32))
        factor = lax.rsqrt(squares / float(cols * n_mp) + epsilon)
        norm_out[:, pl.ds(pl.multiple_of(src * rows, rows), rows)] = gbuf[src] * factor

    def left(ref, sem):
        remote(ref, ref, sem, q_recv, mp=me).wait_send()

    left(sbuf.at[pl.ds(0, n_mp - 1)], z_send)
    for k in range(n_a - 1):
        left(sbuf, a_send.at[k])
    for k in range(n_a * (n_b - 1)):
        left(sbuf, b_send.at[k])
    left(xmax.at[pl.ds(0, n_mp - 1)], m_send)
    left(psend.at[pl.ds(0, n_mp - 1)], p_send)
    left(gbuf.at[pl.ds(0, n_rows - 1)], g_send)
    left(everyone, q_send)


def per_device(n_mp, n_rows, inputs, weight):
    rows, inner = inputs.shape
    cols, inner_all = weight.shape
    quarter = cols // n_rows
    f32, bf16 = jnp.float32, jnp.bfloat16
    n_b = 2 if n_rows % 2 == 0 else 1
    n_a = n_rows // n_b
    dma = pltpu.SemaphoreType.DMA
    vmem = pl.BlockSpec(memory_space=pltpu.VMEM)
    scale, product, normalized = pl.pallas_call(
        functools.partial(kernel, n_mp, n_rows),
        out_shape=(jax.ShapeDtypeStruct((1, rows), f32),
                   jax.ShapeDtypeStruct((cols, rows), f32),
                   jax.ShapeDtypeStruct((cols, rows * n_rows), f32)),
        in_specs=[pl.BlockSpec(memory_space=pl.ANY)] * 2,
        out_specs=(vmem, vmem, vmem),
        scratch_shapes=[
            pltpu.VMEM((quarter, inner_all), f32),
            pltpu.VMEM((cols, inner_all), f32),
            pltpu.VMEM((rows, inner), f32),
            pltpu.VMEM((n_mp, 2, quarter, inner), bf16),
            pltpu.VMEM((n_mp, 2, cols, inner), bf16),
            pltpu.VMEM((2, rows, inner), bf16),
            pltpu.VMEM((n_mp, 1, rows), f32),
            pltpu.VMEM((n_mp, cols, rows), f32),
            pltpu.VMEM((n_mp, cols, rows), f32),
            pltpu.VMEM((n_rows, cols, rows), f32),
            pltpu.VMEM((n_mp * n_rows, 1, rows), f32),
            pltpu.VMEM((cols, 128), f32),
            dma((3,)), dma, dma((n_mp,)),
            dma((max(n_a - 1, 1),)), dma((max(n_a - 1, 1), n_mp)),
            dma((max(n_a * (n_b - 1), 1),)), dma((max(n_a * (n_b - 1), 1), n_mp)),
            dma, dma, dma, dma, dma, dma((max(n_rows - 1, 1),)), dma, dma,
        ],
        compiler_params=pltpu.CompilerParams(
            collective_id=0, has_side_effects=True, vmem_limit_bytes=60 * 2**20
        ),
        name="split_product",
    )(inputs, weight)
    return scale.reshape(rows), product, normalized


def solution(mesh):
    return jax.shard_map(
        functools.partial(per_device, mesh.shape["mp"], mesh.shape["rows"]),
        mesh=mesh,
        in_specs=(P("rows", "mp"), P("mp", None)),
        out_specs=(P("rows"), P("mp", "rows"), P("mp", None)),
        check_vma=False,
    )
```

time: 283 us -> 68.2 us (0.24)
  blocking collectives: 110 us -> 0 us
  waiting for transfers between devices: 78.6 us -> 0 us
  Pallas kernels: 0 us -> 63 us
  local copies, waits for them, and re-layouts: 58.7 us -> 4.38 us
  between operations: 14.1 us -> 0.64 us
  other arithmetic: 8.76 us -> 0 us
  starting transfers between devices: 7.48 us -> 0 us
  matrix products: 3.54 us -> 0 us
    pmax x1 -> x0, blocking collectives: 85 us -> none  [per_device(): row_scale = lax.pmax(jnp.max(jnp.abs(inputs), axis=1), 'mp') + epsilon]
    reduce_scatter x1 -> x0, waiting for transfers between devices: 70.5 us -> none  [per_device(): lax.psum_scatter(partial_term, 'mp', scatter_dimension=0, tiled=True)]
    pallas_call x0 -> x1, Pallas kernels: none -> 63 us  [per_device(): pl.pallas_call(functools.partial(kernel, n_mp, n_rows), out_shape=(jax.Sh...]
    psum x1 -> x0, blocking collectives: 19.4 us -> none  [per_device(): squares = lax.psum(jnp.sum(product * product, axis=0), 'mp')]
    unnamed x9 -> x3, local copies, waits for them, and re-layouts: 22.3 us -> 4.38 us
    another operation x1 -> x0, local copies, waits for them, and re-layouts: 17.8 us -> none  [per_device(): stacked = jnp.stack(w_parts, axis=0)]
    all_to_all x1 -> x0, local copies, waits for them, and re-layouts: 13.6 us -> none  [per_device(): lax.all_to_all(stacked, 'mp', split_axis=2, concat_axis=1, tiled=True)]
    all_to_all x1 -> x0, waiting for transfers between devices: 8.12 us -> none  [per_device(): lax.all_to_all(stacked, 'mp', split_axis=2, concat_axis=1, tiled=True)]
  transfers between devices with their start and end apart: 2 -> 0, of which waited for: 2 -> 0; matrix products, arithmetic and copies ran while one was open for 0% -> 0% of each run, Pallas kernels for 0% -> 0%
where the time goes in v1:
time: 68.2 us; the launch traced here: 68 us
  Pallas kernels  63 us (92%)
  local copies, waits for them, and re-layouts  4.38 us (6%)
    pallas_call x1, Pallas kernels, per_device(): pl.pallas_call(functools.partial(kernel, n_mp, n_rows), out_shape=(jax.Sh...  63 us
    unnamed x3, local copies, waits for them, and re-layouts  4.38 us

profile of v1, /device:TPU:0, one launch (start us, length us, event | category | flops | bytes accessed | tf_op | source)
XLA Modules:
  0.0 68.0 jit_solution(15053506877892884187)
XLA Ops:
  0.6 63.0 %split_product.1 = (f32[1,256]{1,0:T(1,128)}, f32[64,256]{1,0:T(8,128)}, f32[64,1024]{1,0:T(8,128)}) custom-call(f32[256,2048]{1,0:T(8,128)} %x_hbm.1, f32[64,16384]{1,0:T(8,128)} %w_hbm.1), custom_call_target="tpu_custom_call" | custom-call | tf_op jit(solution)/shard_map/split_product/pallas_call | solution.py:258
  63.6 1.2 %copy.8 = f32[256]{0:T(256)} copy(f32[256]{0:T(256)} %bitcast.1) | data formatting | bytes 2048
  64.9 1.5 %copy.9 = f32[64,256]{1,0:T(8,128)} copy(f32[64,256]{1,0:T(8,128)} %get-tuple-element.13) | data formatting | bytes 131072
  66.4 1.7 %copy.10 = f32[64,1024]{1,0:T(8,128)} copy(f32[64,1024]{1,0:T(8,128)} %get-tuple-element.14) | data formatting | bytes 524288

commit v2 on v1

v2 whole, which is shorter than its diff:
```python
import functools

import jax
import jax.numpy as jnp
from jax import lax
from jax.experimental import pallas as pl
from jax.experimental.pallas import tpu as pltpu
from jax.sharding import PartitionSpec as P

epsilon = 1e-06
MESH = pl.DeviceIdType.MESH


def partner(me, step, count):
    if count & (count - 1):
        return lax.rem(step - me + count, count)
    out, bit = 0, 1
    while bit < count:
        out = out + bit * lax.rem(lax.div(me, bit) + lax.div(step, bit), 2)
        bit *= 2
    return out


def kernel(n_mp, n_rows, x_hbm, w_hbm, scale_out, product_out, norm_out,
           wv, xv, sbuf, wbuf, xparts, xmax, psend, pbuf, gbuf, ssq, cscale,
           load_sem, z_send, z_recv, a_send, a_recv, b_send, b_recv,
           m_send, m_recv, p_send, p_recv, g_send, g_recv, q_send, q_recv):
    me, row = lax.axis_index("mp"), lax.axis_index("rows")
    n_b = 2 if n_rows % 2 == 0 else 1
    n_a = n_rows // n_b
    a, b = lax.div(row, n_b), lax.rem(row, n_b)
    total = n_mp * n_rows
    here = me * n_rows + row
    cols, inner_all = wv.shape
    rows, inner = xv.shape
    quarter = cols // n_rows

    half = cols // n_b
    share_at = b * n_a + a
    even = not (n_mp & (n_mp - 1)) and n_mp >= 4
    near = n_mp // 2 if even else n_mp
    fourth = n_mp // 4
    middle = lax.rem(lax.div(me + fourth, near), 2) if even else 0

    def load(at, index):
        rows_at = pl.ds(pl.multiple_of(at * half, half), half)
        return pltpu.make_async_copy(w_hbm.at[rows_at], wv.at[rows_at], load_sem.at[index])

    loads = [load(lax.rem(b + k, n_b), 1 + k) for k in range(n_b)]
    load_x = pltpu.make_async_copy(x_hbm, xv, load_sem.at[0])
    loads[0].start()
    load_x.start()
    for other in loads[1:]:
        other.start()

    barrier = pltpu.get_barrier_semaphore()

    def greet(i, carry):
        to = lax.rem(here + i, total)
        pl.semaphore_signal(barrier, inc=1,
                            device_id={"mp": lax.div(to, n_rows), "rows": lax.rem(to, n_rows)},
                            device_id_type=MESH)
        return carry

    lax.fori_loop(1, total, greet, 0)

    def other_mp(step):
        return partner(me, step, n_mp) if even else lax.rem(me + step, n_mp)

    lanes = 128

    def scale_of(at, count):
        def widest(i, big):
            first = pl.multiple_of(i * inner, inner)
            for j in range(inner // lanes):
                big = jnp.maximum(big, jnp.abs(wv[pl.ds(at, count), pl.ds(first + j * lanes, lanes)]))
            return big

        big = lax.fori_loop(0, n_mp, widest, jnp.zeros((count, lanes), jnp.float32))
        cscale[pl.ds(at, count)] = jnp.broadcast_to(
            jnp.max(big, axis=1, keepdims=True) + epsilon, (count, lanes))

    def cut(at, count, block):
        inverse = 128.0 / cscale[pl.ds(at, count), :1]
        t = wv[pl.ds(at, count), pl.ds(pl.multiple_of(block * inner, inner), inner)] * inverse
        first = jnp.floor(t)
        return first.astype(jnp.bfloat16), jnp.floor((t - first) * 256.0).astype(jnp.bfloat16)

    loads[0].wait()
    half_at = pl.multiple_of(b * half, half)
    quarter_at = pl.multiple_of(share_at * quarter, quarter)
    scale_of(half_at, half)

    def piece(who, at):
        return wbuf.at[who, :, pl.ds(pl.multiple_of(at * quarter, quarter), quarter), :]

    def wide_piece(who, at):
        return wbuf.at[who, :, pl.ds(pl.multiple_of(at * half, half), half), :]

    def remote(src, dst, send, recv, **where):
        return pltpu.make_async_remote_copy(src_ref=src, dst_ref=dst, send_sem=send, recv_sem=recv,
                                            device_id=where, device_id_type=MESH)

    pl.semaphore_wait(barrier, total - 1)

    def send_block(i, carry):
        step = lax.rem(i + middle * near, n_mp)
        to = other_mp(step)

        @pl.when((step > 0) & (step < near))
        def _():
            first, second = cut(half_at, half, to)
            sbuf[to, 0] = first
            sbuf[to, 1] = second
            remote(sbuf.at[to], wide_piece(me, b), z_send.at[0], z_recv.at[me], mp=to).start()

        @pl.when(step >= near)
        def _():
            first, second = cut(quarter_at, quarter, to)
            sbuf[to, 0, :quarter] = first
            sbuf[to, 1, :quarter] = second
            remote(sbuf.at[to, :, pl.ds(0, quarter), :], piece(me, share_at), z_send.at[1],
                   z_recv.at[me], mp=to).start()
        return carry

    lax.fori_loop(0, n_mp, send_block, 0)

    def peer_a(k):
        return lax.rem(a + k, n_a) * n_b + b

    def peer_b(k):
        return a * n_b + lax.rem(b + k, n_b)

    def from_mp(i):
        if not even:
            return i, lax.rem(me - i + n_mp, n_mp)
        group, rest = lax.div(i, fourth), lax.rem(i, fourth)
        odd, high = lax.rem(group, 2), lax.div(group, 2)
        step = (odd * 2 + high + middle * odd * (1 - 2 * high)) * fourth + rest
        return step, other_mp(step)

    load_x.wait()
    peak = jnp.zeros((rows, lanes), jnp.float32)
    for j in range(inner // lanes):
        peak = jnp.maximum(peak, jnp.abs(xv[:, j * lanes:(j + 1) * lanes]))
    xmax[me] = jnp.max(peak.T, axis=0, keepdims=True)

    def tell(i, carry):
        to = lax.rem(me + i, n_mp)
        remote(xmax.at[me], xmax.at[me], m_send, m_recv, mp=to).start()
        return carry

    lax.fori_loop(1, n_mp, tell, 0)

    for k in range(1, n_b):
        loads[k].wait()
        scale_of(pl.multiple_of(lax.rem(b + k, n_b) * half, half), half)
    for k in range(n_b):
        first, second = cut(k * half, half, me)
        wbuf[me, 0, k * half:(k + 1) * half] = first
        wbuf[me, 1, k * half:(k + 1) * half] = second

    def slices_of_x():
        remote(xmax.at[pl.ds(0, n_mp - 1)], xmax.at[pl.ds(0, n_mp - 1)], m_send, m_recv, mp=me).wait_recv()
        row_scale = jnp.max(xmax[...], axis=0) + epsilon
        scale_out[...] = row_scale
        tall = jnp.broadcast_to(128.0 / row_scale, (lanes, rows)).T
        for j in range(inner // lanes):
            at = slice(j * lanes, (j + 1) * lanes)
            t = xv[:, at] * tall
            first = jnp.floor(t)
            xparts[0, :, at] = first.astype(jnp.bfloat16)
            xparts[1, :, at] = jnp.floor((t - first) * 256.0).astype(jnp.bfloat16)

    def dot(w_side, x_side):
        return lax.dot_general(w_side, x_side, (((1,), (1,)), ((), ())),
                               preferred_element_type=jnp.float32)

    wide_at = n_a * (n_b - 1)

    def stage(i, carry):
        @pl.when(i < n_mp)
        def _():
            step, who = from_mp(i)

            @pl.when((step > 0) & (step < near))
            def _():
                got = wide_piece(who, b)
                remote(got, got, z_send.at[0], z_recv.at[who], mp=me).wait_recv()
                for kb in range(1, n_b):
                    remote(got, got, b_send.at[wide_at + kb - 1], b_recv.at[(kb - 1) * n_a, who],
                           rows=peer_b(kb)).start()

            @pl.when(step >= near)
            def _():
                got = piece(who, share_at)
                remote(got, got, z_send.at[1], z_recv.at[who], mp=me).wait_recv()
                for k in range(1, n_a):
                    remote(got, got, a_send.at[k - 1], a_recv.at[k - 1, who], rows=peer_a(k)).start()
                for kb in range(1, n_b):
                    remote(got, got, b_send.at[(kb - 1) * n_a], b_recv.at[(kb - 1) * n_a, who],
                           rows=peer_b(kb)).start()

        @pl.when((i >= 1) & (i < n_mp + 1))
        def _():
            step, who = from_mp(i - 1)

            @pl.when(step >= near)
            def _():
                for k in range(1, n_a):
                    got = piece(who, b * n_a + lax.rem(a - k + n_a, n_a))
                    remote(got, got, a_send.at[k - 1], a_recv.at[k - 1, who], mp=me).wait_recv()
                    for kb in range(1, n_b):
                        at = (kb - 1) * n_a + k
                        remote(got, got, b_send.at[at], b_recv.at[at, who], rows=peer_b(kb)).start()

        @pl.when(i == 2)
        def _():
            slices_of_x()

        @pl.when(i >= 2)
        def _():
            step, who = from_mp(i - 2)

            @pl.when((step > 0) & (step < near))
            def _():
                for kb in range(1, n_b):
                    got = wide_piece(who, lax.rem(b - kb + n_b, n_b))
                    remote(got, got, b_send.at[wide_at + kb - 1], b_recv.at[(kb - 1) * n_a, who],
                           mp=me).wait_recv()

            @pl.when(step >= near)
            def _():
                for kb in range(1, n_b):
                    other_b = lax.rem(b - kb + n_b, n_b)
                    for k in range(n_a):
                        at = (kb - 1) * n_a + k
                        got = piece(who, other_b * n_a + lax.rem(a - k + n_a, n_a))
                        remote(got, got, b_send.at[at], b_recv.at[at, who], mp=me).wait_recv()
            pair = dot(wbuf[who].reshape(2 * cols, inner), xparts[0])
            cross = dot(wbuf[who, 0], xparts[1])
            psend[who] = pair[:cols] + (pair[cols:] + cross) / 256.0

            @pl.when(who != me)
            def _():
                remote(psend.at[who], pbuf.at[me], p_send, p_recv, mp=who).start()

            @pl.when(who == me)
            def _():
                pbuf[me] = psend[me]
        return carry

    lax.fori_loop(0, n_mp + 2, stage, 0)

    remote(pbuf.at[pl.ds(0, n_mp - 1)], pbuf.at[pl.ds(0, n_mp - 1)], p_send, p_recv, mp=me).wait_recv()
    summed = lax.fori_loop(0, n_mp, lambda i, acc: acc + pbuf[i], jnp.zeros((cols, rows), jnp.float32))
    product = summed * cscale[:, :1] * scale_out[...] / float(inner_all)
    gbuf[row] = product
    ssq[here] = jnp.sum(product * product, axis=0, keepdims=True)

    for k in range(1, n_rows):
        remote(gbuf.at[row], gbuf.at[row], g_send, g_recv.at[k - 1], rows=lax.rem(row + k, n_rows)).start()

    def share(i, carry):
        to = lax.rem(here + i, total)
        remote(ssq.at[here], ssq.at[here], q_send, q_recv,
               mp=lax.div(to, n_rows), rows=lax.rem(to, n_rows)).start()
        return carry

    lax.fori_loop(1, total, share, 0)
    product_out[...] = product
    everyone = ssq.at[pl.ds(0, total - 1)]
    remote(everyone, everyone, q_send, q_recv, mp=me).wait_recv()

    for k in range(n_rows):
        src = lax.rem(row - k + n_rows, n_rows)
        if k:
            remote(gbuf.at[src], gbuf.at[src], g_send, g_recv.at[k - 1], mp=me).wait_recv()
        squares = lax.fori_loop(0, n_mp, lambda i, acc: acc + ssq[i * n_rows + src],
                                jnp.zeros((1, rows), jnp.float32))
        factor = lax.rsqrt(squares / float(cols * n_mp) + epsilon)
        norm_out[:, pl.ds(pl.multiple_of(src * rows, rows), rows)] = gbuf[src] * factor

    def left(ref, sem):
        remote(ref, ref, sem, q_recv, mp=me).wait_send()

    left(sbuf.at[pl.ds(0, near - 1)], z_send.at[0])
    for kb in range(n_b - 1):
        left(sbuf.at[pl.ds(0, near - 1)], b_send.at[wide_at + kb])
    if near < n_mp:
        narrow = sbuf.at[pl.ds(0, n_mp - near), :, pl.ds(0, quarter), :]
        left(narrow, z_send.at[1])
        for k in range(n_a - 1):
            left(narrow, a_send.at[k])
        for k in range(n_a * (n_b - 1)):
            left(narrow, b_send.at[k])
    left(xmax.at[pl.ds(0, n_mp - 1)], m_send)
    left(psend.at[pl.ds(0, n_mp - 1)], p_send)
    left(gbuf.at[pl.ds(0, n_rows - 1)], g_send)
    left(everyone, q_send)


def hand_over(scale, product, normalized, scale_out, product_out, norm_out):
    scale_out[...] = scale[...]
    product_out[...] = product[...]
    norm_out[...] = normalized[...]


def per_device(n_mp, n_rows, inputs, weight):
    rows, inner = inputs.shape
    cols, inner_all = weight.shape
    quarter = cols // n_rows
    f32, bf16 = jnp.float32, jnp.bfloat16
    n_b = 2 if n_rows % 2 == 0 else 1
    n_a = n_rows // n_b
    dma = pltpu.SemaphoreType.DMA
    vmem = pl.BlockSpec(memory_space=pltpu.VMEM)
    scale, product, normalized = pl.pallas_call(
        functools.partial(kernel, n_mp, n_rows),
        out_shape=(jax.ShapeDtypeStruct((1, rows), f32),
                   jax.ShapeDtypeStruct((cols, rows), f32),
                   jax.ShapeDtypeStruct((cols, rows * n_rows), f32)),
        in_specs=[pl.BlockSpec(memory_space=pl.ANY)] * 2,
        out_specs=(vmem, vmem, vmem),
        scratch_shapes=[
            pltpu.VMEM((cols, inner_all), f32),
            pltpu.VMEM((rows, inner), f32),
            pltpu.VMEM((n_mp, 2, cols // n_b, inner), bf16),
            pltpu.VMEM((n_mp, 2, cols, inner), bf16),
            pltpu.VMEM((2, rows, inner), bf16),
            pltpu.VMEM((n_mp, 1, rows), f32),
            pltpu.VMEM((n_mp, cols, rows), f32),
            pltpu.VMEM((n_mp, cols, rows), f32),
            pltpu.VMEM((n_rows, cols, rows), f32),
            pltpu.VMEM((n_mp * n_rows, 1, rows), f32),
            pltpu.VMEM((cols, 128), f32),
            dma((1 + n_b,)), dma((2,)), dma((n_mp,)),
            dma((max(n_a - 1, 1),)), dma((max(n_a - 1, 1), n_mp)),
            dma((max((n_a + 1) * (n_b - 1), 1),)), dma((max(n_a * (n_b - 1), 1), n_mp)),
            dma, dma, dma, dma, dma, dma((max(n_rows - 1, 1),)), dma, dma,
        ],
        compiler_params=pltpu.CompilerParams(
            collective_id=0, has_side_effects=True, vmem_limit_bytes=60 * 2**20
        ),
        name="split_product",
    )(inputs, weight)
    scale, product, normalized = pl.pallas_call(
        hand_over,
        out_shape=tuple(jax.ShapeDtypeStruct(each.shape, f32) for each in (scale, product, normalized)),
        in_specs=[vmem] * 3,
        out_specs=(vmem, vmem, vmem),
        name="hand_over",
    )(scale, product, normalized)
    return scale.reshape(rows), product, normalized


def solution(mesh):
    return jax.shard_map(
        functools.partial(per_device, mesh.shape["mp"], mesh.shape["rows"]),
        mesh=mesh,
        in_specs=(P("rows", "mp"), P("mp", None)),
        out_specs=(P("rows"), P("mp", "rows"), P("mp", None)),
        check_vma=False,
    )
```

time: 68.2 us -> 67.9 us (level)
  local copies, waits for them, and re-layouts: 4.38 us -> 0 us
  Pallas kernels: 63 us -> 67.2 us
    unnamed x3 -> x0, local copies, waits for them, and re-layouts: 4.38 us -> none
    pallas_call x1, Pallas kernels: 63 us -> 65.4 us  [per_device(): pl.pallas_call(functools.partial(kernel, n_mp, n_rows), out_shape=(jax.Sh...]
    pallas_call x0 -> x1, Pallas kernels: none -> 1.73 us  [per_device(): pl.pallas_call(hand_over, out_shape=tuple((jax.ShapeDtypeStruct(each.shap...]
where the time goes in v2:
time: 67.9 us; the launch traced here: 67.8 us
  Pallas kernels  67.2 us (99%)
    pallas_call x1, Pallas kernels, per_device(): pl.pallas_call(functools.partial(kernel, n_mp, n_rows), out_shape=(jax.Sh...  65.4 us
    pallas_call x1, Pallas kernels, per_device(): pl.pallas_call(hand_over, out_shape=tuple((jax.ShapeDtypeStruct(each.shap...  1.73 us

profile of v2, /device:TPU:0, one launch (start us, length us, event | category | flops | bytes accessed | tf_op | source)
XLA Modules:
  0.0 67.8 jit_solution(12991558630123045647)
XLA Ops:
  0.6 65.4 %split_product.1 = (f32[1,256]{1,0:T(1,128)}, f32[64,256]{1,0:T(8,128)}, f32[64,1024]{1,0:T(8,128)}) custom-call(f32[256,2048]{1,0:T(8,128)} %x_hbm.1, f32[64,16384]{1,0:T(8,128)} %w_hbm.1), custom_call_target="tpu_custom_call" | custom-call | tf_op jit(solution)/shard_map/split_product/pallas_call | solution.py:318
  66.1 1.7 %hand_over.1 = (f32[1,256]{1,0:T(1,128)}, f32[64,256]{1,0:T(8,128)}, f32[64,1024]{1,0:T(8,128)}) custom-call(f32[1,256]{1,0:T(1,128)} %get-tuple-element.9.scale, f32[64,256]{1,0:T(8,128)} %get-tuple-element.10.product, f32[64,1024]{1,0:T(8,128)} %get-tuple-element.11.normalized), custom_call_target="tpu_custom_call" | custom-call | tf_op jit(solution)/shard_map/hand_over/pallas_call | solution.py:347

commit v3 on v1

--- a/solution.py
+++ b/solution.py
@@ -244,6 +244,12 @@
     left(psend.at[pl.ds(0, n_mp - 1)], p_send)
     left(gbuf.at[pl.ds(0, n_rows - 1)], g_send)
     left(everyone, q_send)
+
+
+def hand_over(scale, product, normalized, scale_out, product_out, norm_out):
+    scale_out[...] = scale[...]
+    product_out[...] = product[...]
+    norm_out[...] = normalized[...]
 
 
 def per_device(n_mp, n_rows, inputs, weight):
@@ -285,6 +291,13 @@
         ),
         name="split_product",
     )(inputs, weight)
+    scale, product, normalized = pl.pallas_call(
+        hand_over,
+        out_shape=tuple(jax.ShapeDtypeStruct(each.shape, f32) for each in (scale, product, normalized)),
+        in_specs=[vmem] * 3,
+        out_specs=(vmem, vmem, vmem),
+        name="hand_over",
+    )(scale, product, normalized)
     return scale.reshape(rows), product, normalized
 
 

time: 68.2 us -> 65.5 us (0.960)
  local copies, waits for them, and re-layouts: 4.38 us -> 0 us
  Pallas kernels: 63 us -> 64.7 us
    unnamed x3 -> x0, local copies, waits for them, and re-layouts: 4.38 us -> none
    pallas_call x0 -> x1, Pallas kernels: none -> 1.73 us  [per_device(): pl.pallas_call(hand_over, out_shape=tuple((jax.ShapeDtypeStruct(each.shap...]
where the time goes in v3:
time: 65.5 us; the launch traced here: 65.4 us
  Pallas kernels  64.7 us (99%)
    pallas_call x1, Pallas kernels, per_device(): pl.pallas_call(functools.partial(kernel, n_mp, n_rows), out_shape=(jax.Sh...  63 us
    pallas_call x1, Pallas kernels, per_device(): pl.pallas_call(hand_over, out_shape=tuple((jax.ShapeDtypeStruct(each.shap...  1.73 us

profile of v3, /device:TPU:0, one launch (start us, length us, event | category | flops | bytes accessed | tf_op | source)
XLA Modules:
  0.0 65.4 jit_solution(17854964239411965923)
XLA Ops:
  0.6 63.0 %split_product.1 = (f32[1,256]{1,0:T(1,128)}, f32[64,256]{1,0:T(8,128)}, f32[64,1024]{1,0:T(8,128)}) custom-call(f32[256,2048]{1,0:T(8,128)} %x_hbm.1, f32[64,16384]{1,0:T(8,128)} %w_hbm.1), custom_call_target="tpu_custom_call" | custom-call | tf_op jit(solution)/shard_map/split_product/pallas_call | solution.py:264
  63.6 1.7 %hand_over.1 = (f32[1,256]{1,0:T(1,128)}, f32[64,256]{1,0:T(8,128)}, f32[64,1024]{1,0:T(8,128)}) custom-call(f32[1,256]{1,0:T(1,128)} %get-tuple-element.9.scale, f32[64,256]{1,0:T(8,128)} %get-tuple-element.10.product, f32[64,1024]{1,0:T(8,128)} %get-tuple-element.11.normalized), custom_call_target="tpu_custom_call" | custom-call | tf_op jit(solution)/shard_map/hand_over/pallas_call | solution.py:294
